TPU v7x, 32 devices: a whole 2x2x4 slice. The times are simulated.
32 devices in a mesh: dp: 8 (over z, core), mp: 4 (over y, x).
Axes of the slice: x: 2, y: 2, z: 4, core: 2. Of those that a mesh axis runs over, the one named last changes fastest.
Arguments:
- features: bfloat16 [8192, 8192], P('dp', 'mp'), may hold values from -6 to 6
- v_weight: bfloat16 [3, 8192, 1024], P(None, 'mp', 'dp'), may hold values from -0.0625 to 0.0625
- u_weight: bfloat16 [3, 1024, 8192], P(None, 'dp', 'mp'), may hold values from -0.1875 to 0.1875
- cross_bias: float32 [3, 8192], P(None, 'mp'), may hold values from -3 to 3
Outputs:
- crossed: bfloat16 [8192, 8192], P('dp', 'mp')
All inputs are finite; a program needn't handle non-finite values.
Results may differ from a plain program's by a relative error of at most 0.009.
Values may be sent and summed in bfloat16 or wider, within the bound.
A program may use at most 128 MiB of HBM per device.

v0:
```python
import jax
import jax.numpy as jnp
from jax import lax
from jax.sharding import PartitionSpec as P


def local(features, v_weight, u_weight, cross_bias):
    carried = features
    layers = v_weight.shape[0]
    for layer_number in range(layers):
        current = carried
        partial_value = jnp.dot(
            current,
            lax.all_gather(v_weight[layer_number], "dp", axis=1, tiled=True),
            preferred_element_type=jnp.float32,
        )
        rank_proj = lax.psum(partial_value, "mp").astype(jnp.bfloat16)
        cross_term = jnp.dot(
            rank_proj,
            lax.all_gather(u_weight[layer_number], "dp", axis=0, tiled=True),
            preferred_element_type=jnp.float32,
        )
        cross_term = cross_term + cross_bias[layer_number]
        carried = (features.astype(jnp.float32) * cross_term + current.astype(jnp.float32)).astype(
            jnp.bfloat16
        )
    return carried


def solution(mesh):
    return jax.shard_map(
        local,
        mesh=mesh,
        in_specs=(P("dp", "mp"), P(None, "mp", "dp"), P(None, "dp", "mp"), P(None, "mp")),
        out_specs=P("dp", "mp"),
        check_vma=False,
    )
```

profile of v0, /device:TPU:0, one launch (start us, length us, event | category | flops | bytes accessed | tf_op | source)
XLA Modules:
  0.0 553.8 jit_solution(13807894456703240402)
XLA Ops:
  6.5 0.0 copy-start
  6.5 0.0 copy-start.1
  6.5 0.0 all-gather.13.cloned.1.call-start
  6.5 2.6 fusion.26
  9.2 0.0 all-gather.13.cloned.1.call-update
  9.2 0.0 all-gather.15.cloned.1.call-start
  9.3 0.0 copy-done
  9.3 1.2 fusion.27
  10.5 0.0 all-gather.15.cloned.1.call-update
  10.5 0.0 all-gather.17.cloned.1.call-start
  10.6 0.7 all-gather.17.cloned.1.call-update
  11.2 0.0 all-gather.19.cloned.1.call-start
  11.3 0.5 all-gather.19.cloned.1.call-update
  11.8 0.0 all-gather.21.cloned.1.call-start
  11.9 0.5 all-gather.21.cloned.1.call-update
  12.4 0.0 all-gather.23.cloned.1.call-start
  12.5 0.5 all-gather.23.cloned.1.call-update
  13.0 0.0 copy-done.1
  13.0 46.9 %all-gather.13.cloned.1.call-done = bf16[1,2048,1024]{2,1,0:T(8,128)(2,1)} async-done(((bf16[1,2048,128]{2,1,0:T(8,128)(2,1)}), bf16[1,2048,1024]{2,1,0:T(8,128)(2,1)}) %all-gather.13.cloned.1.call-update) | async-done | bytes 4194320 | tf_op jit(solution)/shard_map/all_gather | solution.py:14
  59.9 10.0 %fusion.15 = f32[1024,1024]{1,0:T(8,128)} fusion(bf16[1024,2048]{1,0:T(8,128)(2,1)} %param.4, bf16[1,2048,1024]{2,1,0:T(8,128)(2,1)} %all-gather.13.cloned.1.call-done), kind=kOutput, calls=%fused_computation.19 | convolution fusion | flops 4294967296 | bytes 12582912 | tf_op jit(solution)/shard_map/dot_general | solution.py:12
  69.9 145.6 %all-reduce.3 = bf16[1024,1024]{1,0:T(8,128)(2,1)S(1)} all-reduce(f32[1024,1024]{1,0:T(8,128)} %fusion.15), channel_id=1, replica_groups=mesh['dp'=8,'mp'=4] {'mp'}, use_global_device_ids=true, to_apply=%region_0.0 | all-reduce | flops 1048576 | bytes 6291456 | tf_op jit(solution)/shard_map/psum | solution.py:17
  215.5 0.0 all-gather.15.cloned.1.call-done
  215.6 9.2 %fusion = bf16[1024,2048]{1,0:T(8,128)(2,1)} fusion(bf16[1024,2048]{1,0:T(8,128)(2,1)} %param.4, f32[2048]{0:T(1024)S(1)} %bitcast.35, bf16[1,1024,2048]{2,1,0:T(8,128)(2,1)} %all-gather.15.cloned.1.call-done, bf16[1024,1024]{1,0:T(8,128)(2,1)S(1)} %all-reduce.3), kind=kOutput, calls=%fused_computation.4 | convolution fusion | flops 4305453056 | bytes 14688256 | tf_op jit(solution)/shard_map/dot_general | solution.py:18
  224.8 0.0 all-gather.17.cloned.1.call-done
  224.8 10.0 %fusion.11 = f32[1024,1024]{1,0:T(8,128)} fusion(bf16[1024,2048]{1,0:T(8,128)(2,1)} %fusion, bf16[1,2048,1024]{2,1,0:T(8,128)(2,1)} %all-gather.17.cloned.1.call-done), kind=kOutput, calls=%fused_computation.15 | convolution fusion | flops 4294967296 | bytes 12582912 | tf_op jit(solution)/shard_map/dot_general | solution.py:12
  234.8 142.2 %all-reduce.4 = bf16[1024,1024]{1,0:T(8,128)(2,1)S(1)} all-reduce(f32[1024,1024]{1,0:T(8,128)} %fusion.11), channel_id=1, replica_groups=mesh['dp'=8,'mp'=4] {'mp'}, use_global_device_ids=true, to_apply=%region_1.0 | all-reduce | flops 1048576 | bytes 6291456 | tf_op jit(solution)/shard_map/psum | solution.py:17
  377.1 0.0 all-gather.19.cloned.1.call-done
  377.1 9.9 %fusion.2 = bf16[1024,2048]{1,0:T(8,128)(2,1)} fusion(bf16[1024,2048]{1,0:T(8,128)(2,1)} %param.4, bf16[1024,2048]{1,0:T(8,128)(2,1)} %fusion, f32[2048]{0:T(1024)S(1)} %bitcast.34, bf16[1,1024,2048]{2,1,0:T(8,128)(2,1)} %all-gather.19.cloned.1.call-done, bf16[1024,1024]{1,0:T(8,128)(2,1)S(1)} %all-reduce.4), kind=kOutput, calls=%fused_computation.6 | convolution fusion | flops 4307550208 | bytes 18882560 | tf_op jit(solution)/shard_map/dot_general | solution.py:18
  387.0 0.0 all-gather.21.cloned.1.call-done
  387.0 9.9 %fusion.7 = f32[1024,1024]{1,0:T(8,128)} fusion(bf16[1024,2048]{1,0:T(8,128)(2,1)} %fusion.2, bf16[1,2048,1024]{2,1,0:T(8,128)(2,1)} %all-gather.21.cloned.1.call-done), kind=kOutput, calls=%fused_computation.11 | convolution fusion | flops 4294967296 | bytes 12582912 | tf_op jit(solution)/shard_map/dot_general | solution.py:12
  396.9 140.1 %all-reduce.5 = bf16[1024,1024]{1,0:T(8,128)(2,1)S(1)} all-reduce(f32[1024,1024]{1,0:T(8,128)} %fusion.7), channel_id=1, replica_groups=mesh['dp'=8,'mp'=4] {'mp'}, use_global_device_ids=true, to_apply=%region_2.0 | all-reduce | flops 1048576 | bytes 6291456 | tf_op jit(solution)/shard_map/psum | solution.py:17
  537.0 0.0 all-gather.23.cloned.1.call-done
  537.1 9.9 %fusion.4 = bf16[1024,2048]{1,0:T(8,128)(2,1)} fusion(bf16[1024,2048]{1,0:T(8,128)(2,1)} %param.4, bf16[1024,2048]{1,0:T(8,128)(2,1)} %fusion.2, f32[2048]{0:T(1024)S(1)} %bitcast.33, bf16[1,1024,2048]{2,1,0:T(8,128)(2,1)} %all-gather.23.cloned.1.call-done, bf16[1024,1024]{1,0:T(8,128)(2,1)S(1)} %all-reduce.5), kind=kOutput, calls=%fused_computation.8 | convolution fusion | flops 4307550208 | bytes 18882560 | tf_op jit(solution)/shard_map/dot_general | solution.py:18
  (1 shorter events, 0.0 us)
Async XLA Ops:
  6.5 2.7 copy-start
  6.5 6.4 %copy-start.1 = (f32[3,2048]{1,0:T(4,128)S(1)}, f32[3,2048]{1,0:T(4,128)}, u32[]{:S(2)}) copy-start(f32[3,2048]{1,0:T(4,128)} %param.7) | copy-start | bytes 73732
  6.5 53.4 %all-gather.13.cloned.1.call-start = ((), (), s32[]{:S(2)}) async-start(), calls=%async_computation | async-start | bytes 4718592 | tf_op jit(solution)/shard_map/all_gather | solution.py:14
  9.2 206.3 %all-gather.15.cloned.1.call-start = ((), (), s32[]{:S(2)}) async-start(), calls=%async_computation.1 | async-start | bytes 4718592 | tf_op jit(solution)/shard_map/all_gather | solution.py:20
  10.5 214.3 %all-gather.17.cloned.1.call-start = ((), (), s32[]{:S(2)}) async-start(), calls=%async_computation.2 | async-start | bytes 4718592 | tf_op jit(solution)/shard_map/all_gather | solution.py:14
  11.2 365.8 %all-gather.19.cloned.1.call-start = ((), (), s32[]{:S(2)}) async-start(), calls=%async_computation.3 | async-start | bytes 4718592 | tf_op jit(solution)/shard_map/all_gather | solution.py:20
  11.8 375.1 %all-gather.21.cloned.1.call-start = ((), (), s32[]{:S(2)}) async-start(), calls=%async_computation.4 | async-start | bytes 4718592 | tf_op jit(solution)/shard_map/all_gather | solution.py:14
  12.4 524.6 %all-gather.23.cloned.1.call-start = ((), (), s32[]{:S(2)}) async-start(), calls=%async_computation.5 | async-start | bytes 4718592 | tf_op jit(solution)/shard_map/all_gather | solution.py:20
Sparse Core Ops, SparseCore 0:
  9.3 50.5 all-gather.12
  61.5 45.0 all-gather.14
  108.2 46.6 all-gather.16
  156.3 45.0 all-gather.18
  202.8 46.6 all-gather.20
  250.9 45.0 all-gather.22
where the time goes:
time: 554 us
  blocking collectives  428 us (77%)
  matrix products  58.9 us (11%)
  waiting for transfers between devices  49.3 us (9%)
  between operations  13.5 us (2%)
    psum x3, blocking collectives, local(): rank_proj = lax.psum(partial_value, 'mp').astype(jnp.bfloat16)  428 us
    all_gather x3, waiting for transfers between devices, local(): lax.all_gather(v_weight[layer_number], 'dp', axis=1, tiled=True)  46.9 us
    dot_general x3, matrix products, local(): jnp.dot(current, lax.all_gather(v_weight[layer_number], 'dp', axis=1, til...  29.9 us
    dot_general x3, matrix products, local(): jnp.dot(rank_proj, lax.all_gather(u_weight[layer_number], 'dp', axis=0, t...  29 us
  transfers between devices with their start and end apart: 6, of which 1 were waited for; matrix products, arithmetic and copies ran while one was open for 9% of the time, Pallas kernels for 0%

commit v1 on v0

v1 whole, which is shorter than its diff:
```python
import functools

import jax
import jax.numpy as jnp
from jax import lax
from jax.experimental import pallas as pl
from jax.experimental.pallas import tpu as pltpu
from jax.sharding import PartitionSpec as P

MESH = pl.DeviceIdType.MESH
HOPS = (2, -2, 1, -1)


def kernel(nz, n, vt_ref, u_ref, f_ref, b_ref, out_ref, w, pf, sbuf, rbuf, rank,
           loc, zsend, zrecv, fsend, psend, precv, rs_s, rs_r, ag_s, ag_r):
    layers, rs, cols = vt_ref.shape
    rows = f_ref.shape[0]
    seg = rows // n
    ck = 2 * rs
    dp, me = lax.axis_index("dp"), lax.axis_index("mp")
    z, c = dp // 2, dp % 2
    step = jnp.where(2 * z < nz, 1, -1)

    def dev(zt, ct, m):
        return {"dp": zt * 2 + ct, "mp": m}

    def copy_to(src, dst, send, recv, device):
        return pltpu.make_async_remote_copy(
            src_ref=src, dst_ref=dst, send_sem=send, recv_sem=recv,
            device_id=device, device_id_type=MESH)

    def order(i):
        return lax.rem(z + step * i + nz, nz)

    def valid(d):
        return (z + d >= 0) & (z + d < nz)

    def blk(p, s, cc):
        return w.at[p, pl.ds(pl.multiple_of((s * 2 + cc) * rs, rs), rs)]

    def local_copy(p):
        src = (vt_ref if p % 2 == 0 else u_ref).at[p // 2]
        return pltpu.make_async_copy(src, blk(p, z, c), loc.at[p])

    def direct(p, k):
        return copy_to(blk(p, z, c), blk(p, z, c), zsend.at[p, k], zrecv.at[p, z],
                       dev(z + HOPS[k], c, me))

    def arrival(p, s):
        return copy_to(blk(p, s, c), blk(p, s, c), fsend.at[p, s], zrecv.at[p, s], dev(z, 1 - c, me))

    def relays(s):
        return ((s >= z + 2) & (z >= 1)) | ((s <= z - 2) & (z <= nz - 2))

    def relay(p, s):
        return copy_to(blk(p, s, c), blk(p, s, c), fsend.at[p, s], zrecv.at[p, s],
                       dev(jnp.where(s > z, z - 1, z + 1), c, me))

    def push(p, s):
        return copy_to(blk(p, s, c), blk(p, s, c), psend.at[p, s], precv.at[p, s], dev(z, 1 - c, me))

    def pushed(p, s):
        return copy_to(blk(p, s, 1 - c), blk(p, s, 1 - c), psend.at[p, s], precv.at[p, s],
                       dev(z, 1 - c, me))

    def issue_own(p):
        local_copy(p).wait()
        for k in range(len(HOPS)):
            @pl.when(valid(HOPS[k]))
            def _():
                direct(p, k).start()

    def take(p, s):
        @pl.when(s != z)
        def _():
            arrival(p, s).wait_recv()

        @pl.when(relays(s))
        def _():
            relay(p, s).start()

        push(p, s).start()

    def lanes(s):
        return pl.ds(pl.multiple_of(s * ck, ck), ck)

    def seg_rows(m):
        return pl.ds(pl.multiple_of(m * seg, seg), seg)

    def other(k):
        return lax.rem(me + k, n)

    for p in range(2 * layers):
        local_copy(p).start()
    barrier = pltpu.get_barrier_semaphore()
    for k in range(1, n):
        pl.semaphore_signal(barrier, inc=1, device_id=dev(z, c, other(k)), device_id_type=MESH)
    pl.semaphore_signal(barrier, inc=1, device_id=dev(z, 1 - c, me), device_id_type=MESH)
    for d in HOPS:
        @pl.when(valid(d))
        def _():
            pl.semaphore_signal(barrier, inc=1, device_id=dev(z + d, c, me), device_id_type=MESH)
    pl.semaphore_wait(barrier, n + jnp.minimum(z, 2) + jnp.minimum(nz - 1 - z, 2))

    issue_own(0)
    issue_own(1)

    for l in range(layers):
        pv, pu = 2 * l, 2 * l + 1
        cur = f_ref if l == 0 else out_ref

        def sum_out(s, k):
            t = other(k)
            return copy_to(sbuf.at[seg_rows(t), lanes(s)], rbuf.at[l, me, :, lanes(s)],
                           rs_s.at[s, k - 1], rs_r.at[s, me], dev(z, c, t))

        def sum_in(s, k):
            q = other(k)
            return copy_to(sbuf.at[seg_rows(q), lanes(s)], rbuf.at[l, q, :, lanes(s)],
                           rs_s.at[s, k - 1], rs_r.at[s, q], dev(z, c, q))

        def rank_out(s, k):
            mine = rank.at[l, seg_rows(me), lanes(s)]
            return copy_to(mine, mine, ag_s.at[s, k - 1], ag_r.at[s, me], dev(z, c, other(k)))

        def rank_in(s, k):
            q = other(k)
            theirs = rank.at[l, seg_rows(q), lanes(s)]
            return copy_to(theirs, theirs, ag_s.at[s, k - 1], ag_r.at[s, q], dev(z, c, q))

        def reduce(s):
            acc = pf[seg_rows(me), lanes(s)]
            for k in range(1, n):
                sum_in(s, k).wait_recv()
                acc = acc + rbuf[l, other(k), :, lanes(s)].astype(jnp.float32)
            rank[l, seg_rows(me), lanes(s)] = acc.astype(jnp.bfloat16)
            for k in range(1, n):
                rank_out(s, k).start()

        @pl.loop(0, nz)
        def _(i):
            s = order(i)
            take(pv, s)
            pushed(pv, s).wait_recv()
            part = lax.dot_general(cur[...], w[pv, lanes(s), :], (((1,), (1,)), ((), ())),
                                   preferred_element_type=jnp.float32)
            pf[:, lanes(s)] = part
            sbuf[:, lanes(s)] = part.astype(jnp.bfloat16)
            for k in range(1, n):
                sum_out(s, k).start()

            @pl.when(i > 0)
            def _():
                reduce(order(i - 1))

        if pv + 2 < 2 * layers:
            issue_own(pv + 2)
        reduce(order(nz - 1))

        @pl.loop(0, nz)
        def _(i):
            take(pu, order(i))

        if pu + 2 < 2 * layers:
            issue_own(pu + 2)

        @pl.loop(0, nz)
        def _(i):
            s = order(i)
            pushed(pu, s).wait_recv()
            for k in range(1, n):
                rank_in(s, k).wait_recv()

        cb = 256 if cols % 256 == 0 else cols

        @pl.loop(0, cols // cb)
        def _(j):
            at = pl.ds(pl.multiple_of(j * cb, cb), cb)
            cross = jnp.dot(rank[l], w[pu, :, at], preferred_element_type=jnp.float32)
            cross = cross + b_ref[l, at][None, :]
            out_ref[:, at] = (f_ref[:, at].astype(jnp.float32) * cross
                              + cur[:, at].astype(jnp.float32)).astype(jnp.bfloat16)

        @pl.loop(0, nz)
        def _(s):
            for k in range(1, n):
                sum_out(s, k).wait_send()
                rank_out(s, k).wait_send()

    for p in range(2 * layers):
        for k in range(len(HOPS)):
            @pl.when(valid(HOPS[k]))
            def _():
                direct(p, k).wait_send()

        @pl.loop(0, nz)
        def _(s):
            push(p, s).wait_send()

            @pl.when(relays(s))
            def _():
                relay(p, s).wait_send()


def solution(mesh):
    n = mesh.shape["mp"]
    nz = mesh.shape["dp"] // 2

    def local(features, v_weight, u_weight, cross_bias):
        layers, rs, cols = u_weight.shape
        rows = features.shape[0]
        r = rs * nz * 2
        pieces = 2 * layers
        vt = jnp.swapaxes(v_weight, 1, 2)
        vm = pl.BlockSpec(memory_space=pltpu.VMEM)
        hbm = pl.BlockSpec(memory_space=pl.ANY)
        dma = pltpu.SemaphoreType.DMA
        return pl.pallas_call(
            functools.partial(kernel, nz, n),
            out_shape=jax.ShapeDtypeStruct((rows, cols), jnp.bfloat16),
            in_specs=[hbm, hbm, vm, vm],
            out_specs=vm,
            scratch_shapes=[
                pltpu.VMEM((pieces, r, cols), jnp.bfloat16),
                pltpu.VMEM((rows, r), jnp.float32),
                pltpu.VMEM((rows, r), jnp.bfloat16),
                pltpu.VMEM((layers, n, rows // n, r), jnp.bfloat16),
                pltpu.VMEM((layers, rows, r), jnp.bfloat16),
                dma((pieces,)), dma((pieces, len(HOPS))), dma((pieces, nz)), dma((pieces, nz)),
                dma((pieces, nz)), dma((pieces, nz)),
                dma((nz, n)), dma((nz, n)), dma((nz, n)), dma((nz, n)),
            ],
            compiler_params=pltpu.CompilerParams(
                collective_id=0, has_side_effects=True, vmem_limit_bytes=67043328),
            name="cross_layers",
        )(vt, u_weight, features, cross_bias)

    return jax.shard_map(
        local,
        mesh=mesh,
        in_specs=(P("dp", "mp"), P(None, "mp", "dp"), P(None, "dp", "mp"), P(None, "mp")),
        out_specs=P("dp", "mp"),
        check_vma=False,
    )
```

time: 554 us -> 255 us (0.46)
  blocking collectives: 428 us -> 0 us
  Pallas kernels: 0 us -> 248 us
  matrix products: 58.9 us -> 0 us
  waiting for transfers between devices: 49.3 us -> 0 us
  between operations: 13.5 us -> 0.01 us
    psum x3 -> x0, blocking collectives: 428 us -> none  [local(): rank_proj = lax.psum(partial_value, 'mp').astype(jnp.bfloat16)]
    pallas_call x0 -> x1, Pallas kernels: none -> 248 us  [local(): pl.pallas_call(functools.partial(kernel, nz, n), out_shape=jax.ShapeDtype...]
    dot_general x6 -> x0, matrix products: 58.9 us -> none  [the longest x3 29.9 us: local(): jnp.dot(current, lax.all_gather(v_weight[layer_number], 'dp', axis=1, til...]
    all_gather x6 -> x0, waiting for transfers between devices: 47 us -> none  [the longest x3 46.9 us: local(): lax.all_gather(v_weight[layer_number], 'dp', axis=1, tiled=True)]
    unnamed x4 -> x2, local copies, waits for them, and re-layouts: 0.01 us -> 7.37 us
  transfers between devices with their start and end apart: 6 -> 0, of which waited for: 1 -> 0; matrix products, arithmetic and copies ran while one was open for 9% -> 0% of each run, Pallas kernels for 0% -> 0%
where the time goes in v1:
time: 255 us
  Pallas kernels  248 us (97%)
  local copies, waits for them, and re-layouts  7.37 us (3%)
    pallas_call x1, Pallas kernels, local(): pl.pallas_call(functools.partial(kernel, nz, n), out_shape=jax.ShapeDtype...  248 us
    unnamed x2, local copies, waits for them, and re-layouts  7.37 us

profile of v1, /device:TPU:0, one launch (start us, length us, event | category | flops | bytes accessed | tf_op | source)
XLA Modules:
  0.0 255.1 jit_solution(9030510341669871348)
XLA Ops:
  0.0 2.6 %copy.5 = bf16[3,2048,128]{1,2,0:T(8,128)(2,1)} copy(bf16[3,2048,128]{2,1,0:T(8,128)(2,1)} %param.5) | data formatting | bytes 3145728 | tf_op args[1]
  2.6 247.7 %cross_layers.1 = bf16[1024,2048]{1,0:T(8,128)(2,1)} custom-call(bf16[3,128,2048]{2,1,0:T(8,128)(2,1)} %bitcast.1, bf16[3,128,2048]{2,1,0:T(8,128)(2,1)} %u_ref.1, bf16[1024,2048]{1,0:T(8,128)(2,1)} %f_ref.1, f32[3,2048]{1,0:T(4,128)} %b_ref.1), custom_call_target="tpu_custom_call" | custom-call | tf_op jit(solution)/shard_map/cross_layers/pallas_call | solution.py:218
  250.3 4.8 %copy.7 = bf16[1024,2048]{1,0:T(8,128)(2,1)} copy(bf16[1024,2048]{1,0:T(8,128)(2,1)} %cross_layers.1) | data formatting | bytes 8388608

commit v2 on v1

--- a/solution.py
+++ b/solution.py
@@ -8,15 +8,16 @@
 from jax.sharding import PartitionSpec as P
 
 MESH = pl.DeviceIdType.MESH
-HOPS = (2, -2, 1, -1)
-
-
-def kernel(nz, n, vt_ref, u_ref, f_ref, b_ref, out_ref, w, pf, sbuf, rbuf, rank,
-           loc, zsend, zrecv, fsend, psend, precv, rs_s, rs_r, ag_s, ag_r):
-    layers, rs, cols = vt_ref.shape
-    rows = f_ref.shape[0]
+HOPS = (1, -1)
+
+
+def kernel(nz, n, native, v_ref, u_ref, x_ref, b_ref, y_ref, wv, wu, f_ref, out_ref, pf, sbuf, rbuf,
+           rank, loc, zsend, zrecv, fsend, psend, precv, rs_s, rs_r, ag_s, ag_r, in_s, out_s):
+    layers, rs, cols = u_ref.shape
+    rows = x_ref.shape[0]
     seg = rows // n
     ck = 2 * rs
+    cb = 256 if cols % 256 == 0 else cols
     dp, me = lax.axis_index("dp"), lax.axis_index("mp")
     z, c = dp // 2, dp % 2
     step = jnp.where(2 * z < nz, 1, -1)
@@ -30,16 +31,21 @@
             device_id=device, device_id_type=MESH)
 
     def order(i):
-        return lax.rem(z + step * i + nz, nz)
+        near = jnp.minimum(z, nz - 1 - z)
+        zigzag = jnp.where(i % 2 == 1, -((i + 1) // 2), i // 2)
+        return z + step * jnp.where(i <= 2 * near, zigzag, i - near)
 
     def valid(d):
         return (z + d >= 0) & (z + d < nz)
 
     def blk(p, s, cc):
-        return w.at[p, pl.ds(pl.multiple_of((s * 2 + cc) * rs, rs), rs)]
+        if native and p % 2 == 0:
+            return wv.at[p // 2, s, :, pl.ds(pl.multiple_of(cc * rs, rs), rs)]
+        w = wu if p % 2 else wv
+        return w.at[p // 2, pl.ds(pl.multiple_of((s * 2 + cc) * rs, rs), rs)]
 
     def local_copy(p):
-        src = (vt_ref if p % 2 == 0 else u_ref).at[p // 2]
+        src = (v_ref if p % 2 == 0 else u_ref).at[p // 2]
         return pltpu.make_async_copy(src, blk(p, z, c), loc.at[p])
 
     def direct(p, k):
@@ -50,7 +56,7 @@
         return copy_to(blk(p, s, c), blk(p, s, c), fsend.at[p, s], zrecv.at[p, s], dev(z, 1 - c, me))
 
     def relays(s):
-        return ((s >= z + 2) & (z >= 1)) | ((s <= z - 2) & (z <= nz - 2))
+        return ((s > z) & (z >= 1)) | ((s < z) & (z <= nz - 2))
 
     def relay(p, s):
         return copy_to(blk(p, s, c), blk(p, s, c), fsend.at[p, s], zrecv.at[p, s],
@@ -63,10 +69,14 @@
         return copy_to(blk(p, s, 1 - c), blk(p, s, 1 - c), psend.at[p, s], precv.at[p, s],
                        dev(z, 1 - c, me))
 
-    def issue_own(p):
-        local_copy(p).wait()
+    def held(d):
+        return (z >= 1) & (z <= nz - 2)
+
+    def issue_own(p, first):
         for k in range(len(HOPS)):
-            @pl.when(valid(HOPS[k]))
+            hold = held(HOPS[k])
+
+            @pl.when(valid(HOPS[k]) & (jnp.logical_not(hold) if first else hold))
             def _():
                 direct(p, k).start()
 
@@ -90,8 +100,14 @@
     def other(k):
         return lax.rem(me + k, n)
 
+    def block_out(j):
+        at = pl.ds(pl.multiple_of(j * cb, cb), cb)
+        return pltpu.make_async_copy(out_ref.at[:, at], y_ref.at[:, at], out_s.at[j])
+
+    whole_in = pltpu.make_async_copy(x_ref, f_ref, in_s)
     for p in range(2 * layers):
         local_copy(p).start()
+    whole_in.start()
     barrier = pltpu.get_barrier_semaphore()
     for k in range(1, n):
         pl.semaphore_signal(barrier, inc=1, device_id=dev(z, c, other(k)), device_id_type=MESH)
@@ -100,10 +116,14 @@
         @pl.when(valid(d))
         def _():
             pl.semaphore_signal(barrier, inc=1, device_id=dev(z + d, c, me), device_id_type=MESH)
-    pl.semaphore_wait(barrier, n + jnp.minimum(z, 2) + jnp.minimum(nz - 1 - z, 2))
-
-    issue_own(0)
-    issue_own(1)
+    pl.semaphore_wait(barrier, n + jnp.minimum(z, 1) + jnp.minimum(nz - 1 - z, 1))
+
+    for p in range(2 * layers):
+        local_copy(p).wait()
+        issue_own(p, True)
+        if p < 2:
+            issue_own(p, False)
+    whole_in.wait()
 
     for l in range(layers):
         pv, pu = 2 * l, 2 * l + 1
@@ -142,8 +162,11 @@
             s = order(i)
             take(pv, s)
             pushed(pv, s).wait_recv()
-            part = lax.dot_general(cur[...], w[pv, lanes(s), :], (((1,), (1,)), ((), ())),
-                                   preferred_element_type=jnp.float32)
+            if native:
+                part = jnp.dot(cur[...], wv[l, s], preferred_element_type=jnp.float32)
+            else:
+                part = lax.dot_general(cur[...], wv[l, lanes(s), :], (((1,), (1,)), ((), ())),
+                                       preferred_element_type=jnp.float32)
             pf[:, lanes(s)] = part
             sbuf[:, lanes(s)] = part.astype(jnp.bfloat16)
             for k in range(1, n):
@@ -154,7 +177,7 @@
                 reduce(order(i - 1))
 
         if pv + 2 < 2 * layers:
-            issue_own(pv + 2)
+            issue_own(pv + 2, False)
         reduce(order(nz - 1))
 
         @pl.loop(0, nz)
@@ -162,7 +185,7 @@
             take(pu, order(i))
 
         if pu + 2 < 2 * layers:
-            issue_own(pu + 2)
+            issue_own(pu + 2, False)
 
         @pl.loop(0, nz)
         def _(i):
@@ -171,15 +194,21 @@
             for k in range(1, n):
                 rank_in(s, k).wait_recv()
 
-        cb = 256 if cols % 256 == 0 else cols
 
         @pl.loop(0, cols // cb)
         def _(j):
             at = pl.ds(pl.multiple_of(j * cb, cb), cb)
-            cross = jnp.dot(rank[l], w[pu, :, at], preferred_element_type=jnp.float32)
+            cross = jnp.dot(rank[l], wu[l, :, at], preferred_element_type=jnp.float32)
             cross = cross + b_ref[l, at][None, :]
             out_ref[:, at] = (f_ref[:, at].astype(jnp.float32) * cross
                               + cur[:, at].astype(jnp.float32)).astype(jnp.bfloat16)
+            if l == layers - 1:
+                @pl.when(j > 0)
+                def _():
+                    block_out(j - 1).start()
+
+        if l == layers - 1:
+            block_out(cols // cb - 1).start()
 
         @pl.loop(0, nz)
         def _(s):
@@ -200,6 +229,10 @@
             @pl.when(relays(s))
             def _():
                 relay(p, s).wait_send()
+
+    @pl.loop(0, cols // cb)
+    def _(j):
+        block_out(j).wait()
 
 
 def solution(mesh):
@@ -211,17 +244,21 @@
         rows = features.shape[0]
         r = rs * nz * 2
         pieces = 2 * layers
-        vt = jnp.swapaxes(v_weight, 1, 2)
+        native = rs % 128 == 0
+        v = v_weight if native else jnp.swapaxes(v_weight, 1, 2)
         vm = pl.BlockSpec(memory_space=pltpu.VMEM)
         hbm = pl.BlockSpec(memory_space=pl.ANY)
         dma = pltpu.SemaphoreType.DMA
         return pl.pallas_call(
-            functools.partial(kernel, nz, n),
+            functools.partial(kernel, nz, n, native),
             out_shape=jax.ShapeDtypeStruct((rows, cols), jnp.bfloat16),
-            in_specs=[hbm, hbm, vm, vm],
-            out_specs=vm,
+            in_specs=[hbm, hbm, hbm, vm],
+            out_specs=hbm,
             scratch_shapes=[
-                pltpu.VMEM((pieces, r, cols), jnp.bfloat16),
+                pltpu.VMEM((layers, nz, cols, 2 * rs) if native else (layers, r, cols), jnp.bfloat16),
+                pltpu.VMEM((layers, r, cols), jnp.bfloat16),
+                pltpu.VMEM((rows, cols), jnp.bfloat16),
+                pltpu.VMEM((rows, cols), jnp.bfloat16),
                 pltpu.VMEM((rows, r), jnp.float32),
                 pltpu.VMEM((rows, r), jnp.bfloat16),
                 pltpu.VMEM((layers, n, rows // n, r), jnp.bfloat16),
@@ -229,11 +266,12 @@
                 dma((pieces,)), dma((pieces, len(HOPS))), dma((pieces, nz)), dma((pieces, nz)),
                 dma((pieces, nz)), dma((pieces, nz)),
                 dma((nz, n)), dma((nz, n)), dma((nz, n)), dma((nz, n)),
+                dma, dma((cols // (256 if cols % 256 == 0 else cols),)),
             ],
             compiler_params=pltpu.CompilerParams(
                 collective_id=0, has_side_effects=True, vmem_limit_bytes=67043328),
             name="cross_layers",
-        )(vt, u_weight, features, cross_bias)
+        )(v, u_weight, features, cross_bias)
 
     return jax.shard_map(
         local,

time: 255 us -> 225 us (0.88)
  Pallas kernels: 248 us -> 220 us
  local copies, waits for them, and re-layouts: 7.37 us -> 4.79 us
    pallas_call x1, Pallas kernels: 248 us -> 220 us  [local(): pl.pallas_call(functools.partial(kernel, nz, n, native), out_shape=jax.Sh...]
    unnamed x2 -> x1, local copies, waits for them, and re-layouts: 7.37 us -> 4.79 us
where the time goes in v2:
time: 225 us
  Pallas kernels  220 us (98%)
  local copies, waits for them, and re-layouts  4.79 us (2%)
    pallas_call x1, Pallas kernels, local(): pl.pallas_call(functools.partial(kernel, nz, n, native), out_shape=jax.Sh...  220 us
    unnamed x1, local copies, waits for them, and re-layouts  4.79 us

profile of v2, /device:TPU:0, one launch (start us, length us, event | category | flops | bytes accessed | tf_op | source)
XLA Modules:
  0.0 225.1 jit_solution(3810459461649968985)
XLA Ops:
  0.0 220.3 %cross_layers.1 = bf16[1024,2048]{1,0:T(8,128)(2,1)} custom-call(bf16[3,2048,128]{2,1,0:T(8,128)(2,1)} %v_ref.1, bf16[3,128,2048]{2,1,0:T(8,128)(2,1)} %u_ref.1, bf16[1024,2048]{1,0:T(8,128)(2,1)} %x_ref.1, f32[3,2048]{1,0:T(4,128)} %b_ref.1), custom_call_target="tpu_custom_call" | custom-call | tf_op jit(solution)/shard_map/cross_layers/pallas_call | solution.py:252
  220.3 4.8 %copy.6 = bf16[1024,2048]{1,0:T(8,128)(2,1)} copy(bf16[1024,2048]{1,0:T(8,128)(2,1)} %cross_layers.1) | data formatting | bytes 8388608
